TPU v7x, 32 devices: a whole 2x2x4 slice. The times are simulated.
32 devices in a mesh: sec: 16 (over z, y, x), node: 2 (over core).
Axes of the slice: x: 2, y: 2, z: 4, core: 2. Of those that a mesh axis runs over, the one named last changes fastest.
Arguments:
- env_blocks: bfloat16 [2, 6144, 128, 128], P('node', 'sec'), may hold values from -10 to 10, as said below
- iso_blocks: bfloat16 [2, 6144, 128, 128], P('node', 'sec'), may hold values from -6 to 6
- joined_sector: int32 [2, 6144], P('node', 'sec'), may hold values from 0 to 15, as said below
- owner_map: int32 [2, 16], P('node'), may hold values from 0 to 15, each once within a row
- live_pairs: int32 [2, 16], P('node', 'sec'), may hold values from 1 to 384, as said below
Outputs:
- environment: float32 [2, 16, 128, 128], P('node', 'sec')
Inputs may be any that keep to these rules, and one draw needn't show every extreme that they name: `env_blocks`: each block is symmetric. `joined_sector`: slot p belongs to tree node k = p // 3072 of its group, and its sector is one of that node's sectors k * 8 to k * 8 + 7. `owner_map`: each row names every index once. `live_pairs`: in every group some index of sec has all 384 slots live.
All inputs are finite; a program needn't handle non-finite values.
Results may differ from a plain program's by a relative error of at most 0.0003.
Values sent between devices are 32-bit elements; how exact they have to be, the bound alone decides.
A program may use at most 128 MiB of HBM per device.

v0:
```python
import jax
import jax.numpy as jnp
from jax import lax
from jax.sharding import PartitionSpec as P

pair_group = 32


def body(env_blocks, iso_blocks, joined_sector, owner_map, live_pairs):
    pairs_here = env_blocks.shape[1]
    sector_width = iso_blocks.shape[3]
    sectors = lax.axis_size("sec")
    sector_ids = jnp.arange(sectors, dtype=jnp.int32)
    matches = joined_sector[0][:, None] == sector_ids[None, :]
    targets = jnp.sum(jnp.where(matches, owner_map[0][None, :], 0), axis=1)
    living = jnp.arange(pairs_here, dtype=jnp.int32) < live_pairs[0, 0]

    def add_group(turn_index, partial_value):
        first_pair = turn_index * pair_group
        blocks = lax.dynamic_slice_in_dim(env_blocks[0], first_pair, pair_group, 0)
        weights = lax.dynamic_slice_in_dim(iso_blocks[0], first_pair, pair_group, 0)
        group_targets = lax.dynamic_slice_in_dim(targets, first_pair, pair_group, 0)
        group_live = lax.dynamic_slice_in_dim(living, first_pair, pair_group, 0)
        product = jnp.einsum(
            "prk,pkc->prc", blocks, weights, preferred_element_type=jnp.float32
        ).astype(jnp.bfloat16)
        sandwich = jnp.einsum("prc,prd->pcd", weights, product, preferred_element_type=jnp.float32)
        selector = ((group_targets[:, None] == sector_ids[None, :]) & group_live[:, None]).astype(
            jnp.float32
        )
        flat_terms = sandwich.reshape(pair_group, sector_width * sector_width)
        added = lax.dot_general(
            selector,
            flat_terms,
            (((0,), (0,)), ((), ())),
            precision=lax.Precision.HIGHEST,
            preferred_element_type=jnp.float32,
        )
        return partial_value + added

    zero_sums = jnp.zeros((sectors, sector_width * sector_width), jnp.float32)
    turn_total = (live_pairs[0, 0] + pair_group - 1) // pair_group
    partial_value = lax.fori_loop(0, turn_total, add_group, zero_sums).reshape(
        sectors, sector_width, sector_width
    )
    summed = lax.psum_scatter(partial_value, "sec", scatter_dimension=0, tiled=True)[0]
    hermitian = jnp.triu(summed) + jnp.triu(summed, 1).T
    squares = jnp.sum(hermitian * hermitian)
    grand_total = lax.psum(squares, ("sec", "node"))
    entries = sectors * lax.axis_size("node") * sector_width * sector_width
    factor = lax.rsqrt(grand_total / entries + 1e-06)
    return (hermitian * factor)[None, None]


def solution(mesh):
    in_specs = (
        P("node", "sec", None, None),
        P("node", "sec", None, None),
        P("node", "sec"),
        P("node", None),
        P("node", "sec"),
    )
    out_specs = P("node", "sec", None, None)
    return jax.shard_map(body, mesh=mesh, in_specs=in_specs, out_specs=out_specs, check_vma=False)
```

profile of v0, /device:TPU:0, one launch (start us, length us, event | category | flops | bytes accessed | tf_op | source)
XLA Modules:
  0.0 199.3 jit_solution(596673899991960904)
XLA Ops:
  7.2 0.7 reduce
  7.9 0.7 select_reduce_fusion
  8.7 25.5 %while.11 = (s32[]{:T(128)}, f32[16,16384]{1,0:T(8,128)S(1)}, s32[]{:T(128)}, s32[384]{0:T(512)S(1)}, pred[384]{0:T(512)(128)(4,1)S(1)}, /*index=5*/bf16[1,384,1...) while((s32[]{:T(128)}, f32[16,16384]{1,0:T(8,128)S(1)}, ...), condition=%wide.region_2.3_spmd.clone, body=%wide.region_1.2_spmd.clone.sunk | while | flops 369886208 | bytes 9439363 | solution.py:43
  8.8 2.6 %fusion.30 = f32[32,128,128]{2,1,0:T(8,128)S(1)} fusion(bf16[1,384,128,128]{3,2,1,0:T(8,128)(2,1)} %get-tuple-element.166, s32[]{:T(128)S(6)} %select_n.40, bf16[1,384,128,128]{3,2,1,0:T(8,128)(2,1)} %get-tuple-element.165), kind=kOutput, calls=%fused_computation.5.clone.1 | convolution fusion | flops 268959744 | bytes 5244416 | tf_op jit(solution)/shard_map/while/body/prc,prd->pcd/dot_general | solution.py:27
  11.4 0.1 dynamic_slice.42
  11.5 2.3 %convolution_add_fusion.2 = f32[16,16384]{1,0:T(8,128)S(1)} fusion(f32[16,16384]{1,0:T(8,128)S(1)} %get-tuple-element.150, f32[4,8,128,128]{3,2,1,0:T(8,128)S(1)} %bitcast.39, s32[32]{0:T(128)S(1)} %dynamic_slice.42, pred[32]{0:T(512)(128)(4,1)S(1)} %dynamic_slice.43), kind=kOutput, calls=%fused_computation.1.clone.1 | convolution fusion | flops 100926464 | bytes 4194464 | tf_op jit(solution)/shard_map/while/body/dot_general | solution.py:32
  13.9 2.6 %fusion.30 = f32[32,128,128]{2,1,0:T(8,128)S(1)} fusion(bf16[1,384,128,128]{3,2,1,0:T(8,128)(2,1)} %get-tuple-element.166, s32[]{:T(128)S(6)} %select_n.40, bf16[1,384,128,128]{3,2,1,0:T(8,128)(2,1)} %get-tuple-element.165), kind=kOutput, calls=%fused_computation.5.clone.1 | convolution fusion | flops 268959744 | bytes 5244416 | tf_op jit(solution)/shard_map/while/body/prc,prd->pcd/dot_general | solution.py:27
  16.5 0.1 dynamic_slice.42
  16.6 2.3 %convolution_add_fusion.2 = f32[16,16384]{1,0:T(8,128)S(1)} fusion(f32[16,16384]{1,0:T(8,128)S(1)} %get-tuple-element.150, f32[4,8,128,128]{3,2,1,0:T(8,128)S(1)} %bitcast.39, s32[32]{0:T(128)S(1)} %dynamic_slice.42, pred[32]{0:T(512)(128)(4,1)S(1)} %dynamic_slice.43), kind=kOutput, calls=%fused_computation.1.clone.1 | convolution fusion | flops 100926464 | bytes 4194464 | tf_op jit(solution)/shard_map/while/body/dot_general | solution.py:32
  19.0 2.6 %fusion.30 = f32[32,128,128]{2,1,0:T(8,128)S(1)} fusion(bf16[1,384,128,128]{3,2,1,0:T(8,128)(2,1)} %get-tuple-element.166, s32[]{:T(128)S(6)} %select_n.40, bf16[1,384,128,128]{3,2,1,0:T(8,128)(2,1)} %get-tuple-element.165), kind=kOutput, calls=%fused_computation.5.clone.1 | convolution fusion | flops 268959744 | bytes 5244416 | tf_op jit(solution)/shard_map/while/body/prc,prd->pcd/dot_general | solution.py:27
  21.6 0.1 dynamic_slice.42
  21.7 2.3 %convolution_add_fusion.2 = f32[16,16384]{1,0:T(8,128)S(1)} fusion(f32[16,16384]{1,0:T(8,128)S(1)} %get-tuple-element.150, f32[4,8,128,128]{3,2,1,0:T(8,128)S(1)} %bitcast.39, s32[32]{0:T(128)S(1)} %dynamic_slice.42, pred[32]{0:T(512)(128)(4,1)S(1)} %dynamic_slice.43), kind=kOutput, calls=%fused_computation.1.clone.1 | convolution fusion | flops 100926464 | bytes 4194464 | tf_op jit(solution)/shard_map/while/body/dot_general | solution.py:32
  24.1 2.6 %fusion.30 = f32[32,128,128]{2,1,0:T(8,128)S(1)} fusion(bf16[1,384,128,128]{3,2,1,0:T(8,128)(2,1)} %get-tuple-element.166, s32[]{:T(128)S(6)} %select_n.40, bf16[1,384,128,128]{3,2,1,0:T(8,128)(2,1)} %get-tuple-element.165), kind=kOutput, calls=%fused_computation.5.clone.1 | convolution fusion | flops 268959744 | bytes 5244416 | tf_op jit(solution)/shard_map/while/body/prc,prd->pcd/dot_general | solution.py:27
  26.7 0.1 dynamic_slice.42
  26.8 2.3 %convolution_add_fusion.2 = f32[16,16384]{1,0:T(8,128)S(1)} fusion(f32[16,16384]{1,0:T(8,128)S(1)} %get-tuple-element.150, f32[4,8,128,128]{3,2,1,0:T(8,128)S(1)} %bitcast.39, s32[32]{0:T(128)S(1)} %dynamic_slice.42, pred[32]{0:T(512)(128)(4,1)S(1)} %dynamic_slice.43), kind=kOutput, calls=%fused_computation.1.clone.1 | convolution fusion | flops 100926464 | bytes 4194464 | tf_op jit(solution)/shard_map/while/body/dot_general | solution.py:32
  29.2 2.6 %fusion.30 = f32[32,128,128]{2,1,0:T(8,128)S(1)} fusion(bf16[1,384,128,128]{3,2,1,0:T(8,128)(2,1)} %get-tuple-element.166, s32[]{:T(128)S(6)} %select_n.40, bf16[1,384,128,128]{3,2,1,0:T(8,128)(2,1)} %get-tuple-element.165), kind=kOutput, calls=%fused_computation.5.clone.1 | convolution fusion | flops 268959744 | bytes 5244416 | tf_op jit(solution)/shard_map/while/body/prc,prd->pcd/dot_general | solution.py:27
  31.9 2.3 %convolution_add_fusion.2 = f32[16,16384]{1,0:T(8,128)S(1)} fusion(f32[16,16384]{1,0:T(8,128)S(1)} %get-tuple-element.150, f32[4,8,128,128]{3,2,1,0:T(8,128)S(1)} %bitcast.39, s32[32]{0:T(128)S(1)} %dynamic_slice.42, pred[32]{0:T(512)(128)(4,1)S(1)} %dynamic_slice.43), kind=kOutput, calls=%fused_computation.1.clone.1 | convolution fusion | flops 100926464 | bytes 4194464 | tf_op jit(solution)/shard_map/while/body/dot_general | solution.py:32
  34.2 1.2 copy.19
  35.5 115.3 %reduce-scatter.2.cloned.1.call-done = f32[1,128,128]{2,1,0:T(8,128)} async-done(((f32[16,128,128]{2,1,0:T(8,128)}), f32[1,128,128]{2,1,0:T(8,128)}) %reduce-scatter.2.cloned.1.call-update) | async-done | bytes 65552 | tf_op jit(solution)/shard_map/reduce_scatter | solution.py:46
  150.7 0.9 copy.13
  151.7 1.5 multiply_reduce_fusion
  153.1 37.0 %psum.7 = f32[]{:T(128)} all-reduce(f32[]{:T(128)} %multiply_reduce_fusion), channel_id=1, replica_groups=mesh['sec'=16,'node'=2] {'sec','node'}, use_global_device_ids=true, to_apply=%region_5.6 | all-reduce | flops 1 | bytes 8 | tf_op jit(solution)/shard_map/psum | solution.py:49
  190.8 0.9 multiply_bitcast_fusion
  191.7 0.7 copy.15
  (11 shorter events, 0.6 us)
Async XLA Ops:
  6.5 144.2 %reduce-scatter.2.cloned.1.call-start = ((), (), s32[]{:S(2)}) async-start(), calls=%async_computation.1 | async-start | bytes 1114112 | tf_op jit(solution)/shard_map/reduce_scatter | solution.py:46
Sparse Core Ops, SparseCore 0:
  35.6 115.0 reduce-scatter.1
where the time goes:
time: 201 us; the launch traced here: 199 us
  waiting for transfers between devices  115 us (57%)
  blocking collectives  37 us (18%)
  matrix products  24.5 us (12%)
  between operations  14.8 us (7%)
  other arithmetic  3.79 us (2%)
  local copies, waits for them, and re-layouts  3.69 us (2%)
    reduce_scatter x1, waiting for transfers between devices, body(): lax.psum_scatter(partial_value, 'sec', scatter_dimension=0, tiled=True)[0]  115 us
    psum x1, blocking collectives, body(): grand_total = lax.psum(squares, ('sec', 'node'))  37 us
    dot_general x5, matrix products, add_group(): jnp.einsum('prc,prd->pcd', weights, product, preferred_element_type=jnp.f...  13.1 us
    dot_general x5, matrix products, add_group(): lax.dot_general(selector, flat_terms, (((0,), (0,)), ((), ())), precision...  11.5 us
  transfers between devices with their start and end apart: 1, of which 1 were waited for; matrix products, arithmetic and copies ran while one was open for 0% of the time, Pallas kernels for 0%

commit v1 on v0

v1 whole, which is shorter than its diff:
```python
import functools
import jax
import jax.numpy as jnp
from jax import lax
from jax.experimental import pallas as pl
from jax.experimental.pallas import tpu as pltpu
from jax.sharding import PartitionSpec as P

SECTORS_NODE = 8
CHUNK = 16
AHEAD = 6
UNROLL = 8
MESH = pl.DeviceIdType.MESH


def local_kernel(live_ref, sector_ref, env_ref, iso_ref, out_ref, blocks, weights, sums, sems):
    width = sums.shape[-1]
    half = width // 2
    live = live_ref[0, 0]
    chunks = (live + CHUNK - 1) // CHUNK

    def copies(index):
        where = pl.ds(index * CHUNK, CHUNK)
        return (
            pltpu.make_async_copy(env_ref.at[0, where], blocks.at[where], sems.at[0, index]),
            pltpu.make_async_copy(iso_ref.at[0, where], weights.at[where], sems.at[1, index]),
        )

    def start(index, carry):
        for copy in copies(index):
            copy.start()
        return carry

    lax.fori_loop(0, jnp.minimum(chunks, AHEAD), start, 0)
    sums[...] = jnp.zeros_like(sums)

    def step(index, carry):
        @pl.when(index + AHEAD < chunks)
        def _():
            start(index + AHEAD, 0)

        for copy in copies(index):
            copy.wait()

        def some(part, carry):
            first = index * CHUNK + part * UNROLL
            terms = []
            for k in range(UNROLL):
                w = weights[first + k]
                z = jnp.dot(blocks[first + k], w, preferred_element_type=jnp.float32)
                y = lax.dot_general(
                    w,
                    z.astype(jnp.bfloat16),
                    (((0,), (0,)), ((), ())),
                    preferred_element_type=jnp.float32,
                )
                terms.append(y)
            for k in range(UNROLL):
                slot = first + k
                local = lax.rem(sector_ref[0, slot], SECTORS_NODE)
                place = jnp.where(slot < live, local, SECTORS_NODE)
                sums[place] += terms[k]
            return carry

        return lax.fori_loop(0, CHUNK // UNROLL, some, carry)

    lax.fori_loop(0, chunks, step, 0)

    rows = lax.broadcasted_iota(jnp.int32, (half, width), 0)
    lanes = lax.broadcasted_iota(jnp.int32, (half, width), 1)
    piece = half // SECTORS_NODE
    for s in range(SECTORS_NODE):
        whole = sums[s]
        low = pltpu.roll(whole.T[half:], half, 1)
        packed = jnp.where(lanes >= rows, whole[:half], low)
        diagonal = jnp.sum(
            jnp.where(lanes == rows + half, whole[half:], 0.0), axis=0, keepdims=True
        )
        for c in range(SECTORS_NODE):
            out_ref[c, pl.ds(s * piece, piece)] = packed[c * piece : (c + 1) * piece]
            out_ref[c, pl.ds(half + s, 1)] = diagonal


def exchange_kernel(sec_count, node_count, owner_ref, part_ref, out_ref, first, mine, second,
                    squares, send_one, recv_one, send_two, recv_two, send_sq, recv_sq):
    members = SECTORS_NODE
    width = out_ref.shape[-1]
    half = width // 2
    piece = half // members
    me = lax.axis_index("sec")
    node = lax.axis_index("node")
    base = (me // members) * members
    rank = me - base

    barrier = pltpu.get_barrier_semaphore()
    for o in range(node_count):
        other = lax.rem(node + o, node_count)

        def greet(step, carry, other=other):
            pl.semaphore_signal(
                barrier, inc=1, device_id=(lax.rem(me + step, sec_count), other),
                device_id_type=MESH,
            )
            return carry

        lax.fori_loop(1 if o == 0 else 0, sec_count, greet, 0)
    pl.semaphore_wait(barrier, sec_count * node_count - 1)

    def to_member(step):
        peer = lax.rem(rank + step, members)
        source = lax.rem(rank + members - step, members)
        return peer, source

    def copy_one(slot, peer, step):
        return pltpu.make_async_remote_copy(
            src_ref=part_ref.at[peer], dst_ref=first.at[slot],
            send_sem=send_one.at[step], recv_sem=recv_one.at[slot],
            device_id=(base + peer, node), device_id_type=MESH,
        )

    for step in range(1, members):
        peer, _ = to_member(step)
        copy_one(step, peer, step).start()
    total = part_ref[rank]
    for step in range(1, members):
        peer, _ = to_member(step)
        copy_one(step, peer, step).wait_recv()
        total += first[step]

    shape = (half, width)
    rows = lax.rem(lax.broadcasted_iota(jnp.int32, shape, 0), piece) + rank * piece
    lanes = lax.broadcasted_iota(jnp.int32, shape, 1)
    body = total[:half]
    diagonals = total[half:]
    weight = jnp.where(lanes == rows, 1.0, 2.0)
    tall = lax.broadcasted_iota(jnp.int32, diagonals.shape, 1) - half
    here = (tall >= rank * piece) & (tall < (rank + 1) * piece)
    square = jnp.sum(weight * body * body) + jnp.sum(
        jnp.where(here, diagonals * diagonals, 0.0)
    )
    squares[me * node_count + node] = jnp.full(squares.shape[1:], square, jnp.float32)

    def copy_square(step, o):
        other = lax.rem(node + o, node_count)
        target = lax.rem(me + step, sec_count)
        place = me * node_count + node
        return pltpu.make_async_remote_copy(
            src_ref=squares.at[place], dst_ref=squares.at[place],
            send_sem=send_sq.at[o, step], recv_sem=recv_sq.at[o, step],
            device_id=(target, other), device_id_type=MESH,
        )

    for o in range(node_count):

        def send_square(step, carry, o=o):
            copy_square(step, o).start()
            return carry

        lax.fori_loop(1 if o == 0 else 0, sec_count, send_square, 0)

    def copy_two(step):
        target = lax.rem(me + step, sec_count)
        return pltpu.make_async_remote_copy(
            src_ref=mine.at[target], dst_ref=second.at[me],
            send_sem=send_two.at[step], recv_sem=recv_two.at[step],
            device_id=(target, node), device_id_type=MESH,
        )

    def fill(step, carry):
        target = lax.rem(me + step, sec_count)
        band = jnp.zeros((piece, width), jnp.float32)
        line = jnp.zeros((1, width), jnp.float32)
        for s in range(members):
            hit = jnp.full((piece, width), owner_ref[0, base + s], jnp.int32) == target
            band = jnp.where(hit, body[s * piece : (s + 1) * piece], band)
            line = jnp.where(hit[:1], diagonals[s : s + 1], line)
        mine[target, pl.ds(0, piece)] = band
        mine[target, pl.ds(piece, 1)] = line

        @pl.when(step > 0)
        def _():
            copy_two(step).start()

        return carry

    lax.fori_loop(0, sec_count, fill, 0)
    second[me] = mine[me]

    def take(step, carry):
        copy_two(step).wait_recv()
        return carry

    lax.fori_loop(1, sec_count, take, 0)
    for o in range(node_count):

        def take_square(step, carry, o=o):
            copy_square(step, o).wait_recv()
            return carry

        lax.fori_loop(1 if o == 0 else 0, sec_count, take_square, 0)

    everything = squares[:, :1, :]
    grand = jnp.sum(everything, axis=0)
    factor = lax.rsqrt(grand / (sec_count * node_count * width * width) + 1e-06)
    arrived = []
    for c in range(members):
        whole = second[c]
        for g in range(1, sec_count // members):
            whole += second[g * members + c]
        arrived.append(whole)
    packed = jnp.concatenate([a[:piece] for a in arrived], axis=0)
    diagonal = arrived[0][piece : piece + 1]
    square_form = jnp.concatenate([packed, pltpu.roll(packed, half, 1)], axis=0)
    i = lax.broadcasted_iota(jnp.int32, (width, width), 0)
    j = lax.broadcasted_iota(jnp.int32, (width, width), 1)
    kept = ((i < half) & (j >= i)) | ((j >= half) & (j < i))
    full = jnp.where(kept, square_form, square_form.T)
    full = jnp.where((i == j) & (i >= half), diagonal, full)
    out_ref[0, 0] = full * factor

    for step in range(1, members):
        peer, _ = to_member(step)
        copy_one(step, peer, step).wait_send()

    def sent(step, carry):
        copy_two(step).wait_send()
        return carry

    lax.fori_loop(1, sec_count, sent, 0)
    for o in range(node_count):

        def sent_square(step, carry, o=o):
            copy_square(step, o).wait_send()
            return carry

        lax.fori_loop(1 if o == 0 else 0, sec_count, sent_square, 0)


def local_sums(live_pairs, joined_sector, env_blocks, iso_blocks):
    pairs = env_blocks.shape[1]
    height = env_blocks.shape[2]
    width = iso_blocks.shape[3]
    half = width // 2
    chunks = pairs // CHUNK
    hbm = pl.BlockSpec(memory_space=pl.ANY)
    smem = pl.BlockSpec(memory_space=pltpu.SMEM)
    return pl.pallas_call(
        local_kernel,
        out_shape=jax.ShapeDtypeStruct((SECTORS_NODE, half + SECTORS_NODE, width), jnp.float32),
        in_specs=[smem, smem, hbm, hbm],
        out_specs=pl.BlockSpec(memory_space=pltpu.VMEM),
        scratch_shapes=[
            pltpu.VMEM((pairs, height, height), jnp.bfloat16),
            pltpu.VMEM((pairs, height, width), jnp.bfloat16),
            pltpu.VMEM((SECTORS_NODE + 1, width, width), jnp.float32),
            pltpu.SemaphoreType.DMA((2, chunks)),
        ],
        compiler_params=pltpu.CompilerParams(vmem_limit_bytes=62 * 1024 * 1024),
        name="local_sums",
    )(live_pairs, joined_sector, env_blocks, iso_blocks)


def body(env_blocks, iso_blocks, joined_sector, owner_map, live_pairs):
    width = iso_blocks.shape[3]
    half = width // 2
    piece = half // SECTORS_NODE
    sec_count = lax.axis_size("sec")
    node_count = lax.axis_size("node")
    parts = local_sums(live_pairs, joined_sector, env_blocks, iso_blocks)
    vmem = pl.BlockSpec(memory_space=pltpu.VMEM)
    dma = pltpu.SemaphoreType.DMA
    return pl.pallas_call(
        functools.partial(exchange_kernel, sec_count, node_count),
        out_shape=jax.ShapeDtypeStruct((1, 1, width, width), jnp.float32),
        in_specs=[pl.BlockSpec(memory_space=pltpu.SMEM), vmem],
        out_specs=vmem,
        scratch_shapes=[
            pltpu.VMEM(parts.shape, jnp.float32),
            pltpu.VMEM((sec_count, 2 * piece, width), jnp.float32),
            pltpu.VMEM((sec_count, 2 * piece, width), jnp.float32),
            pltpu.VMEM((sec_count * node_count, 8, width), jnp.float32),
            dma((SECTORS_NODE,)),
            dma((SECTORS_NODE,)),
            dma((sec_count,)),
            dma((sec_count,)),
            dma((node_count, sec_count)),
            dma((node_count, sec_count)),
        ],
        compiler_params=pltpu.CompilerParams(
            collective_id=0, has_side_effects=True, vmem_limit_bytes=8 * 1024 * 1024
        ),
        name="exchange",
    )(owner_map, parts)


def solution(mesh):
    in_specs = (
        P("node", "sec", None, None),
        P("node", "sec", None, None),
        P("node", "sec"),
        P("node", None),
        P("node", "sec"),
    )
    out_specs = P("node", "sec", None, None)
    return jax.shard_map(body, mesh=mesh, in_specs=in_specs, out_specs=out_specs, check_vma=False)
```

time: 201 us -> 46.3 us (0.23)
  waiting for transfers between devices: 115 us -> 0 us
  Pallas kernels: 0 us -> 43.7 us
  blocking collectives: 37 us -> 0 us
  matrix products: 24.5 us -> 0 us
  between operations: 14.8 us -> 0.69 us
  other arithmetic: 3.79 us -> 0 us
  local copies, waits for them, and re-layouts: 3.69 us -> 1.59 us
    reduce_scatter x1 -> x0, waiting for transfers between devices: 115 us -> none  [body(): lax.psum_scatter(partial_value, 'sec', scatter_dimension=0, tiled=True)[0]]
    pallas_call x0 -> x2, Pallas kernels: none -> 43.7 us  [the longest x1 39.4 us: body(): pl.pallas_call(functools.partial(exchange_kernel, sec_count, node_count),...]
    psum x1 -> x0, blocking collectives: 37 us -> none  [body(): grand_total = lax.psum(squares, ('sec', 'node'))]
    dot_general x10 -> x0, matrix products: 24.5 us -> none  [the longest x5 13.1 us: add_group(): jnp.einsum('prc,prd->pcd', weights, product, preferred_element_type=jnp.f...]
    reduce_sum x2 -> x0, other arithmetic: 2.21 us -> none  [the longest x1 1.47 us: body(): squares = jnp.sum(hermitian * hermitian)]
  transfers between devices with their start and end apart: 1 -> 0, of which waited for: 1 -> 0; matrix products, arithmetic and copies ran while one was open for 0% -> 0% of each run, Pallas kernels for 0% -> 0%
where the time goes in v1:
time: 46.3 us; the launch traced here: 46 us
  Pallas kernels  43.7 us (94%)
  local copies, waits for them, and re-layouts  1.59 us (3%)
  between operations  0.69 us (1%)
    pallas_call x1, Pallas kernels, body(): pl.pallas_call(functools.partial(exchange_kernel, sec_count, node_count),...  39.4 us
    pallas_call x1, Pallas kernels, local_sums(): pl.pallas_call(local_kernel, out_shape=jax.ShapeDtypeStruct((SECTORS_NODE...  4.25 us
    unnamed x5, local copies, waits for them, and re-layouts  1.59 us

profile of v1, /device:TPU:0, one launch (start us, length us, event | category | flops | bytes accessed | tf_op | source)
XLA Modules:
  0.0 46.0 jit_solution(17986667444558209263)
XLA Ops:
  0.7 0.0 copy-start.1
  0.7 4.3 %local_sums.1.part_ref = f32[8,72,128]{2,1,0:T(8,128)} custom-call(s32[1,1]{1,0:T(1,128)S(6)} %copy.7.live_ref, s32[1,384]{1,0:T(1,128)} %sector_ref.1, bf16[1,384,128,128]{3,2,1,0:T(8,128)(2,1)} %env_ref.1, bf16[1,384,128,128]{3,2,1,0:T(8,128)(2,1)} %iso_ref.1), custom_call_target="tpu_custom_call" | custom-call | tf_op jit(solution)/shard_map/local_sums/pallas_call | solution.py:247
  4.9 0.0 copy-done.1
  4.9 0.0 copy-start
  4.9 1.0 %copy-done = f32[8,72,128]{2,1,0:T(8,128)S(1)} copy-done((f32[8,72,128]{2,1,0:T(8,128)S(1)}, f32[8,72,128]{2,1,0:T(8,128)}, u32[]{:S(2)}) %copy-start) | copy-done | bytes 294936
  5.9 39.4 %exchange.1 = f32[1,1,128,128]{3,2,1,0:T(8,128)S(1)} custom-call(s32[1,16]{1,0:T(1,128)S(1)} %copy-done.1, f32[8,72,128]{2,1,0:T(8,128)S(1)} %copy-done), custom_call_target="tpu_custom_call" | custom-call | tf_op jit(solution)/shard_map/exchange/pallas_call | solution.py:272
  45.3 0.6 %copy.8 = f32[1,1,128,128]{3,2,1,0:T(8,128)} copy(f32[1,1,128,128]{3,2,1,0:T(8,128)S(1)} %exchange.1) | data formatting | bytes 131072
Async XLA Ops:
  0.7 4.3 %copy-start.1 = (s32[1,16]{1,0:T(1,128)S(1)}, s32[1,16]{1,0:T(1,128)}, u32[]{:S(2)}) copy-start(s32[1,16]{1,0:T(1,128)} %owner_ref.1) | copy-start | bytes 196
  4.9 1.0 %copy-start = (f32[8,72,128]{2,1,0:T(8,128)S(1)}, f32[8,72,128]{2,1,0:T(8,128)}, u32[]{:S(2)}) copy-start(f32[8,72,128]{2,1,0:T(8,128)} %local_sums.1.part_ref) | copy-start | bytes 884740

commit v2 on v1

v2 whole, which is shorter than its diff:
```python
import functools
import jax
import jax.numpy as jnp
from jax import lax
from jax.experimental import pallas as pl
from jax.experimental.pallas import tpu as pltpu
from jax.sharding import PartitionSpec as P

SECTORS_NODE = 8
CHUNK = 32
AHEAD = 4
MESH = pl.DeviceIdType.MESH


def local_kernel(live_ref, sector_ref, env_ref, iso_ref, out_ref, blocks, weights, held, sums, sems):
    width = sums.shape[-1]
    half = width // 2
    live = live_ref[0, 0]
    chunks = (live + CHUNK - 1) // CHUNK

    def copies(index):
        where = pl.ds(index * CHUNK, CHUNK)
        return (
            pltpu.make_async_copy(env_ref.at[0, where], blocks.at[where], sems.at[0, index]),
            pltpu.make_async_copy(iso_ref.at[0, where], weights.at[where], sems.at[1, index]),
        )

    def start(index, carry):
        for copy in copies(index):
            copy.start()
        return carry

    lax.fori_loop(0, jnp.minimum(chunks, AHEAD), start, 0)
    sums[...] = jnp.zeros_like(sums)

    pairs = CHUNK // 2
    zero = jnp.zeros(weights.shape[1:], jnp.bfloat16)

    def diagonal_pair(top, bottom):
        return jnp.concatenate(
            [jnp.concatenate([top, zero], axis=1), jnp.concatenate([zero, bottom], axis=1)],
            axis=0,
        )

    def product(index, k):
        one = index * CHUNK + 2 * k
        two = one + 1
        z = jnp.dot(
            jnp.concatenate([blocks[one], blocks[two]], axis=1),
            diagonal_pair(weights[one], weights[two]),
            preferred_element_type=jnp.float32,
        )
        held[k] = z.astype(jnp.bfloat16)

    def sandwich(index, k):
        one = index * CHUNK + 2 * k
        two = one + 1
        y = lax.dot_general(
            jnp.concatenate([weights[one], weights[two]], axis=0),
            diagonal_pair(held[k, :, :width], held[k, :, width:]),
            (((0,), (0,)), ((), ())),
            preferred_element_type=jnp.float32,
        )
        for slot, term in ((one, y[:, :width]), (two, y[:, width:])):
            local = lax.rem(sector_ref[0, slot], SECTORS_NODE)
            place = jnp.where(slot < live, local, SECTORS_NODE)
            sums[place] += term

    def arrive(index):
        @pl.when(index + AHEAD < chunks)
        def _():
            start(index + AHEAD, 0)

        for copy in copies(index):
            copy.wait()

    def step(index, carry):
        arrive(index)
        for k in range(pairs):
            sandwich(index - 1, k)
            product(index, k)
        return carry

    arrive(0)
    for k in range(pairs):
        product(0, k)
    lax.fori_loop(1, chunks, step, 0)
    for k in range(pairs):
        sandwich(chunks - 1, k)

    rows = lax.broadcasted_iota(jnp.int32, (half, width), 0)
    lanes = lax.broadcasted_iota(jnp.int32, (half, width), 1)
    piece = half // SECTORS_NODE
    for s in range(SECTORS_NODE):
        whole = sums[s]
        low = pltpu.roll(whole.T[half:], half, 1)
        packed = jnp.where(lanes >= rows, whole[:half], low)
        diagonal = jnp.sum(
            jnp.where(lanes == rows + half, whole[half:], 0.0), axis=0, keepdims=True
        )
        for c in range(SECTORS_NODE):
            out_ref[c, pl.ds(s * piece, piece)] = packed[c * piece : (c + 1) * piece]
            out_ref[c, pl.ds(half + s, 1)] = diagonal


def exchange_kernel(sec_count, node_count, owner_ref, part_ref, out_ref, first, bands, mine, second,
                    squares, picks, send_one, recv_one, send_two, recv_two, send_sq, recv_sq):
    members = SECTORS_NODE
    width = out_ref.shape[-1]
    half = width // 2
    piece = half // members
    me = lax.axis_index("sec")
    node = lax.axis_index("node")
    base = (me // members) * members
    rank = me - base

    barrier = pltpu.get_barrier_semaphore()
    for o in range(node_count):
        other = lax.rem(node + o, node_count)

        def greet(step, carry, other=other):
            pl.semaphore_signal(
                barrier, inc=1, device_id=(lax.rem(me + step, sec_count), other),
                device_id_type=MESH,
            )
            return carry

        lax.fori_loop(1 if o == 0 else 0, sec_count, greet, 0)

    def pick(target, carry):
        found = jnp.int32(members)
        for s in range(members):
            found = jnp.where(owner_ref[0, base + s] == target, s, found)
        picks[target] = found
        return carry

    lax.fori_loop(0, sec_count, pick, 0)
    pl.semaphore_wait(barrier, sec_count * node_count - 1)

    def copy_one(step):
        peer = lax.rem(rank + step, members)
        return pltpu.make_async_remote_copy(
            src_ref=part_ref.at[peer], dst_ref=first.at[step],
            send_sem=send_one.at[step], recv_sem=recv_one.at[step],
            device_id=(base + peer, node), device_id_type=MESH,
        )

    for step in range(1, members):
        copy_one(step).start()
    total = part_ref[rank]
    for step in range(1, members):
        copy_one(step).wait_recv()
        total += first[step]

    shape = (half, width)
    rows = lax.rem(lax.broadcasted_iota(jnp.int32, shape, 0), piece) + rank * piece
    lanes = lax.broadcasted_iota(jnp.int32, shape, 1)
    body = total[:half]
    diagonals = total[half:]
    weight = jnp.where(lanes == rows, 1.0, 2.0)
    tall = lax.broadcasted_iota(jnp.int32, diagonals.shape, 1) - half
    here = (tall >= rank * piece) & (tall < (rank + 1) * piece)
    weighted = weight * body * body
    folded = jnp.where(here, diagonals * diagonals, 0.0)
    for s in range(members):
        folded += weighted[s * piece : (s + 1) * piece]
    square = jnp.sum(folded, axis=0, keepdims=True)
    for s in range(members):
        bands[s, pl.ds(0, piece)] = body[s * piece : (s + 1) * piece]
        bands[s, pl.ds(piece, 1)] = diagonals[s : s + 1]
        bands[s, pl.ds(piece + 1, 1)] = square
    bands[members, pl.ds(0, piece + 1)] = jnp.zeros((piece + 1, width), jnp.float32)
    bands[members, pl.ds(piece + 1, 1)] = square

    def copy_two(step):
        target = lax.rem(me + step, sec_count)
        return pltpu.make_async_remote_copy(
            src_ref=mine.at[target], dst_ref=second.at[me],
            send_sem=send_two.at[step], recv_sem=recv_two.at[step],
            device_id=(target, node), device_id_type=MESH,
        )

    def copy_square(step, o):
        return pltpu.make_async_remote_copy(
            src_ref=bands.at[members, pl.ds(piece, 8)], dst_ref=squares.at[o - 1, me],
            send_sem=send_sq.at[o - 1, step], recv_sem=recv_sq.at[o - 1, step],
            device_id=(lax.rem(me + step, sec_count), lax.rem(node + o, node_count)),
            device_id_type=MESH,
        )

    def fill(back, carry):
        step = sec_count - 1 - back
        target = lax.rem(me + step, sec_count)
        mine[target] = bands[picks[target]]

        @pl.when(step > 0)
        def _():
            copy_two(step).start()

        for o in range(1, node_count):
            copy_square(step, o).start()
        return carry

    lax.fori_loop(0, sec_count, fill, 0)
    second[me] = mine[me]

    def take(step, carry):
        copy_two(step).wait_recv()
        return carry

    lax.fori_loop(1, sec_count, take, 0)

    arrived = []
    for c in range(members):
        whole = second[c]
        for g in range(1, sec_count // members):
            whole += second[g * members + c]
        arrived.append(whole)
    packed = jnp.concatenate([a[:piece] for a in arrived], axis=0)
    diagonal = arrived[0][piece : piece + 1]
    grand = arrived[0][piece + 1 : piece + 2]
    for c in range(1, members):
        grand += arrived[c][piece + 1 : piece + 2]
    square_form = jnp.concatenate([packed, pltpu.roll(packed, half, 1)], axis=0)
    i = lax.broadcasted_iota(jnp.int32, (width, width), 0)
    j = lax.broadcasted_iota(jnp.int32, (width, width), 1)
    kept = ((i < half) & (j >= i)) | ((j >= half) & (j < i))
    full = jnp.where(kept, square_form, square_form.T)
    full = jnp.where((i == j) & (i >= half), diagonal, full)

    for o in range(1, node_count):

        def take_square(step, carry, o=o):
            copy_square(step, o).wait_recv()
            return carry

        lax.fori_loop(0, sec_count, take_square, 0)
        grand += jnp.sum(squares[o - 1], axis=0)[1:2]
    mean = jnp.sum(grand, axis=1, keepdims=True) / (sec_count * node_count * width * width)
    out_ref[0, 0] = full * lax.rsqrt(mean + 1e-06)

    for step in range(1, members):
        copy_one(step).wait_send()

    def sent(step, carry):
        copy_two(step).wait_send()
        return carry

    lax.fori_loop(1, sec_count, sent, 0)
    for o in range(1, node_count):

        def sent_square(step, carry, o=o):
            copy_square(step, o).wait_send()
            return carry

        lax.fori_loop(0, sec_count, sent_square, 0)


def local_sums(live_pairs, joined_sector, env_blocks, iso_blocks):
    pairs = env_blocks.shape[1]
    height = env_blocks.shape[2]
    width = iso_blocks.shape[3]
    half = width // 2
    chunks = pairs // CHUNK
    hbm = pl.BlockSpec(memory_space=pl.ANY)
    smem = pl.BlockSpec(memory_space=pltpu.SMEM)
    return pl.pallas_call(
        local_kernel,
        out_shape=jax.ShapeDtypeStruct((SECTORS_NODE, half + SECTORS_NODE, width), jnp.float32),
        in_specs=[smem, smem, hbm, hbm],
        out_specs=pl.BlockSpec(memory_space=pltpu.VMEM),
        scratch_shapes=[
            pltpu.VMEM((pairs, height, height), jnp.bfloat16),
            pltpu.VMEM((pairs, height, width), jnp.bfloat16),
            pltpu.VMEM((CHUNK // 2, height, 2 * width), jnp.bfloat16),
            pltpu.VMEM((SECTORS_NODE + 1, width, width), jnp.float32),
            pltpu.SemaphoreType.DMA((2, chunks)),
        ],
        compiler_params=pltpu.CompilerParams(vmem_limit_bytes=56 * 1024 * 1024),
        name="local_sums",
    )(live_pairs, joined_sector, env_blocks, iso_blocks)


def body(env_blocks, iso_blocks, joined_sector, owner_map, live_pairs):
    width = iso_blocks.shape[3]
    half = width // 2
    piece = half // SECTORS_NODE
    sec_count = lax.axis_size("sec")
    node_count = lax.axis_size("node")
    parts = local_sums(live_pairs, joined_sector, env_blocks, iso_blocks)
    vmem = pl.BlockSpec(memory_space=pltpu.VMEM)
    dma = pltpu.SemaphoreType.DMA
    return pl.pallas_call(
        functools.partial(exchange_kernel, sec_count, node_count),
        out_shape=jax.ShapeDtypeStruct((1, 1, width, width), jnp.float32),
        in_specs=[pl.BlockSpec(memory_space=pltpu.SMEM), vmem],
        out_specs=vmem,
        scratch_shapes=[
            pltpu.VMEM(parts.shape, jnp.float32),
            pltpu.VMEM((SECTORS_NODE + 1, piece + 8, width), jnp.float32),
            pltpu.VMEM((sec_count, piece + 8, width), jnp.float32),
            pltpu.VMEM((sec_count, piece + 8, width), jnp.float32),
            pltpu.VMEM((max(node_count - 1, 1), sec_count, 8, width), jnp.float32),
            pltpu.SMEM((sec_count,), jnp.int32),
            dma((SECTORS_NODE,)),
            dma((SECTORS_NODE,)),
            dma((sec_count,)),
            dma((sec_count,)),
            dma((max(node_count - 1, 1), sec_count)),
            dma((max(node_count - 1, 1), sec_count)),
        ],
        compiler_params=pltpu.CompilerParams(
            collective_id=0, has_side_effects=True, vmem_limit_bytes=8 * 1024 * 1024
        ),
        name="exchange",
    )(owner_map, parts)


def solution(mesh):
    in_specs = (
        P("node", "sec", None, None),
        P("node", "sec", None, None),
        P("node", "sec"),
        P("node", None),
        P("node", "sec"),
    )
    out_specs = P("node", "sec", None, None)
    return jax.shard_map(body, mesh=mesh, in_specs=in_specs, out_specs=out_specs, check_vma=False)
```

time: 46.3 us -> 35.4 us (0.76)
  Pallas kernels: 43.7 us -> 32.9 us
    pallas_call x1, Pallas kernels: 39.4 us -> 25.8 us  [body(): pl.pallas_call(functools.partial(exchange_kernel, sec_count, node_count),...]
    pallas_call x1, Pallas kernels: 4.25 us -> 7.08 us  [local_sums(): pl.pallas_call(local_kernel, out_shape=jax.ShapeDtypeStruct((SECTORS_NODE...]
where the time goes in v2:
time: 35.4 us; the launch traced here: 35.1 us
  Pallas kernels  32.9 us (93%)
  local copies, waits for them, and re-layouts  1.59 us (4%)
  between operations  0.69 us (2%)
    pallas_call x1, Pallas kernels, body(): pl.pallas_call(functools.partial(exchange_kernel, sec_count, node_count),...  25.8 us
    pallas_call x1, Pallas kernels, local_sums(): pl.pallas_call(local_kernel, out_shape=jax.ShapeDtypeStruct((SECTORS_NODE...  7.08 us
    unnamed x5, local copies, waits for them, and re-layouts  1.59 us

profile of v2, /device:TPU:0, one launch (start us, length us, event | category | flops | bytes accessed | tf_op | source)
XLA Modules:
  0.0 35.1 jit_solution(17766962093827550365)
XLA Ops:
  0.7 0.0 copy-start.1
  0.7 7.1 %local_sums.1.part_ref = f32[8,72,128]{2,1,0:T(8,128)} custom-call(s32[1,1]{1,0:T(1,128)S(6)} %copy.7.live_ref, s32[1,384]{1,0:T(1,128)} %sector_ref.1, bf16[1,384,128,128]{3,2,1,0:T(8,128)(2,1)} %env_ref.1, bf16[1,384,128,128]{3,2,1,0:T(8,128)(2,1)} %iso_ref.1), custom_call_target="tpu_custom_call" | custom-call | tf_op jit(solution)/shard_map/local_sums/pallas_call | solution.py:267
  7.7 0.0 copy-done.1
  7.8 0.0 copy-start
  7.8 1.0 %copy-done = f32[8,72,128]{2,1,0:T(8,128)S(1)} copy-done((f32[8,72,128]{2,1,0:T(8,128)S(1)}, f32[8,72,128]{2,1,0:T(8,128)}, u32[]{:S(2)}) %copy-start) | copy-done | bytes 294936
  8.7 25.8 %exchange.1 = f32[1,1,128,128]{3,2,1,0:T(8,128)S(1)} custom-call(s32[1,16]{1,0:T(1,128)S(1)} %copy-done.1, f32[8,72,128]{2,1,0:T(8,128)S(1)} %copy-done), custom_call_target="tpu_custom_call" | custom-call | tf_op jit(solution)/shard_map/exchange/pallas_call | solution.py:293
  34.5 0.6 %copy.8 = f32[1,1,128,128]{3,2,1,0:T(8,128)} copy(f32[1,1,128,128]{3,2,1,0:T(8,128)S(1)} %exchange.1) | data formatting | bytes 131072
Async XLA Ops:
  0.7 7.1 %copy-start.1 = (s32[1,16]{1,0:T(1,128)S(1)}, s32[1,16]{1,0:T(1,128)}, u32[]{:S(2)}) copy-start(s32[1,16]{1,0:T(1,128)} %owner_ref.1) | copy-start | bytes 196
  7.8 1.0 %copy-start = (f32[8,72,128]{2,1,0:T(8,128)S(1)}, f32[8,72,128]{2,1,0:T(8,128)}, u32[]{:S(2)}) copy-start(f32[8,72,128]{2,1,0:T(8,128)} %local_sums.1.part_ref) | copy-start | bytes 884740

commit v3 on v2

--- a/solution.py
+++ b/solution.py
@@ -12,9 +12,9 @@
 MESH = pl.DeviceIdType.MESH
 
 
-def local_kernel(live_ref, sector_ref, env_ref, iso_ref, out_ref, blocks, weights, held, sums, sems):
+def local_kernel(live_ref, sector_hbm, env_ref, iso_ref, sums, blocks, weights, held, sector_ref,
+                 sems, sector_sem):
     width = sums.shape[-1]
-    half = width // 2
     live = live_ref[0, 0]
     chunks = (live + CHUNK - 1) // CHUNK
 
@@ -31,6 +31,8 @@
         return carry
 
     lax.fori_loop(0, jnp.minimum(chunks, AHEAD), start, 0)
+    sector_copy = pltpu.make_async_copy(sector_hbm, sector_ref, sector_sem)
+    sector_copy.start()
     sums[...] = jnp.zeros_like(sums)
 
     pairs = CHUNK // 2
@@ -84,26 +86,13 @@
     arrive(0)
     for k in range(pairs):
         product(0, k)
+    sector_copy.wait()
     lax.fori_loop(1, chunks, step, 0)
     for k in range(pairs):
         sandwich(chunks - 1, k)
 
-    rows = lax.broadcasted_iota(jnp.int32, (half, width), 0)
-    lanes = lax.broadcasted_iota(jnp.int32, (half, width), 1)
-    piece = half // SECTORS_NODE
-    for s in range(SECTORS_NODE):
-        whole = sums[s]
-        low = pltpu.roll(whole.T[half:], half, 1)
-        packed = jnp.where(lanes >= rows, whole[:half], low)
-        diagonal = jnp.sum(
-            jnp.where(lanes == rows + half, whole[half:], 0.0), axis=0, keepdims=True
-        )
-        for c in range(SECTORS_NODE):
-            out_ref[c, pl.ds(s * piece, piece)] = packed[c * piece : (c + 1) * piece]
-            out_ref[c, pl.ds(half + s, 1)] = diagonal
-
-
-def exchange_kernel(sec_count, node_count, owner_ref, part_ref, out_ref, first, bands, mine, second,
+
+def exchange_kernel(sec_count, node_count, owner_ref, sums_ref, out_ref, part_ref, first, bands, mine, second,
                     squares, picks, send_one, recv_one, send_two, recv_two, send_sq, recv_sq):
     members = SECTORS_NODE
     width = out_ref.shape[-1]
@@ -126,6 +115,19 @@
             return carry
 
         lax.fori_loop(1 if o == 0 else 0, sec_count, greet, 0)
+
+    rows = lax.broadcasted_iota(jnp.int32, (half, width), 0)
+    lanes = lax.broadcasted_iota(jnp.int32, (half, width), 1)
+    for s in range(members):
+        whole = sums_ref[s]
+        low = pltpu.roll(whole.T[half:], half, 1)
+        packed = jnp.where(lanes >= rows, whole[:half], low)
+        diagonal = jnp.sum(
+            jnp.where(lanes == rows + half, whole[half:], 0.0), axis=0, keepdims=True
+        )
+        for c in range(members):
+            part_ref[c, pl.ds(s * piece, piece)] = packed[c * piece : (c + 1) * piece]
+            part_ref[c, pl.ds(half + s, 1)] = diagonal
 
     def pick(target, carry):
         found = jnp.int32(members)
@@ -260,23 +262,23 @@
     pairs = env_blocks.shape[1]
     height = env_blocks.shape[2]
     width = iso_blocks.shape[3]
-    half = width // 2
     chunks = pairs // CHUNK
-    hbm = pl.BlockSpec(memory_space=pl.ANY)
+    hbm = pl.BlockSpec(memory_space=pltpu.HBM)
     smem = pl.BlockSpec(memory_space=pltpu.SMEM)
     return pl.pallas_call(
         local_kernel,
-        out_shape=jax.ShapeDtypeStruct((SECTORS_NODE, half + SECTORS_NODE, width), jnp.float32),
-        in_specs=[smem, smem, hbm, hbm],
+        out_shape=jax.ShapeDtypeStruct((SECTORS_NODE + 1, width, width), jnp.float32),
+        in_specs=[smem, hbm, hbm, hbm],
         out_specs=pl.BlockSpec(memory_space=pltpu.VMEM),
         scratch_shapes=[
             pltpu.VMEM((pairs, height, height), jnp.bfloat16),
             pltpu.VMEM((pairs, height, width), jnp.bfloat16),
             pltpu.VMEM((CHUNK // 2, height, 2 * width), jnp.bfloat16),
-            pltpu.VMEM((SECTORS_NODE + 1, width, width), jnp.float32),
+            pltpu.SMEM(joined_sector.shape, jnp.int32),
             pltpu.SemaphoreType.DMA((2, chunks)),
+            pltpu.SemaphoreType.DMA,
         ],
-        compiler_params=pltpu.CompilerParams(vmem_limit_bytes=56 * 1024 * 1024),
+        compiler_params=pltpu.CompilerParams(vmem_limit_bytes=52 * 1024 * 1024),
         name="local_sums",
     )(live_pairs, joined_sector, env_blocks, iso_blocks)
 
@@ -287,7 +289,7 @@
     piece = half // SECTORS_NODE
     sec_count = lax.axis_size("sec")
     node_count = lax.axis_size("node")
-    parts = local_sums(live_pairs, joined_sector, env_blocks, iso_blocks)
+    sums = local_sums(live_pairs, joined_sector, env_blocks, iso_blocks)
     vmem = pl.BlockSpec(memory_space=pltpu.VMEM)
     dma = pltpu.SemaphoreType.DMA
     return pl.pallas_call(
@@ -296,7 +298,8 @@
         in_specs=[pl.BlockSpec(memory_space=pltpu.SMEM), vmem],
         out_specs=vmem,
         scratch_shapes=[
-            pltpu.VMEM(parts.shape, jnp.float32),
+            pltpu.VMEM((SECTORS_NODE, half + SECTORS_NODE, width), jnp.float32),
+            pltpu.VMEM((SECTORS_NODE, half + SECTORS_NODE, width), jnp.float32),
             pltpu.VMEM((SECTORS_NODE + 1, piece + 8, width), jnp.float32),
             pltpu.VMEM((sec_count, piece + 8, width), jnp.float32),
             pltpu.VMEM((sec_count, piece + 8, width), jnp.float32),
@@ -313,7 +316,7 @@
             collective_id=0, has_side_effects=True, vmem_limit_bytes=8 * 1024 * 1024
         ),
         name="exchange",
-    )(owner_map, parts)
+    )(owner_map, sums)
 
 
 def solution(mesh):

time: 35.4 us -> 34.4 us (0.972)
  Pallas kernels: 32.9 us -> 32.2 us
    pallas_call x1, Pallas kernels: 25.8 us -> 22.9 us  [body(): pl.pallas_call(functools.partial(exchange_kernel, sec_count, node_count),...]
    pallas_call x1, Pallas kernels: 7.08 us -> 9.31 us  [local_sums(): pl.pallas_call(local_kernel, out_shape=jax.ShapeDtypeStruct((SECTORS_NODE...]
where the time goes in v3:
time: 34.4 us; the launch traced here: 34.2 us
  Pallas kernels  32.2 us (94%)
  local copies, waits for them, and re-layouts  1.31 us (4%)
  between operations  0.68 us (2%)
    pallas_call x1, Pallas kernels, body(): pl.pallas_call(functools.partial(exchange_kernel, sec_count, node_count),...  22.9 us
    pallas_call x1, Pallas kernels, local_sums(): pl.pallas_call(local_kernel, out_shape=jax.ShapeDtypeStruct((SECTORS_NODE...  9.31 us
    unnamed x5, local copies, waits for them, and re-layouts  1.31 us

profile of v3, /device:TPU:0, one launch (start us, length us, event | category | flops | bytes accessed | tf_op | source)
XLA Modules:
  0.0 34.2 jit_solution(495216964810925916)
XLA Ops:
  0.7 0.0 copy-start
  0.7 0.7 %copy-done = s32[1,384]{1,0:T(1,128)S(1)} copy-done((s32[1,384]{1,0:T(1,128)S(1)}, s32[1,384]{1,0:T(1,128)}, u32[]{:S(2)}) %copy-start) | copy-done | bytes 1560
  1.3 0.0 copy-start.1
  1.3 9.3 %local_sums.1.sums_ref = f32[9,128,128]{2,1,0:T(8,128)S(1)} custom-call(s32[1,1]{1,0:T(1,128)S(6)} %copy.7.live_ref, s32[1,384]{1,0:T(1,128)S(1)} %copy-done, bf16[1,384,128,128]{3,2,1,0:T(8,128)(2,1)} %env_ref.1, bf16[1,384,128,128]{3,2,1,0:T(8,128)(2,1)} %iso_ref.1), custom_call_target="tpu_custom_call" | custom-call | tf_op jit(solution)/shard_map/local_sums/pallas_call | solution.py:268
  10.7 0.0 copy-done.1
  10.7 22.9 %exchange.1 = f32[1,1,128,128]{3,2,1,0:T(8,128)S(1)} custom-call(s32[1,16]{1,0:T(1,128)S(1)} %copy-done.1, f32[9,128,128]{2,1,0:T(8,128)S(1)} %local_sums.1.sums_ref), custom_call_target="tpu_custom_call" | custom-call | tf_op jit(solution)/shard_map/exchange/pallas_call | solution.py:295
  33.5 0.6 %copy.8 = f32[1,1,128,128]{3,2,1,0:T(8,128)} copy(f32[1,1,128,128]{3,2,1,0:T(8,128)S(1)} %exchange.1) | data formatting | bytes 131072
Async XLA Ops:
  0.7 0.7 %copy-start = (s32[1,384]{1,0:T(1,128)S(1)}, s32[1,384]{1,0:T(1,128)}, u32[]{:S(2)}) copy-start(s32[1,384]{1,0:T(1,128)} %sector_hbm.1) | copy-start | bytes 4612
  1.3 9.3 %copy-start.1 = (s32[1,16]{1,0:T(1,128)S(1)}, s32[1,16]{1,0:T(1,128)}, u32[]{:S(2)}) copy-start(s32[1,16]{1,0:T(1,128)} %owner_ref.1) | copy-start | bytes 196
